TPU v7x, 32 devices: a whole 2x2x4 slice. The times are simulated.
32 devices in a mesh: seq: 8 (over z, y), grp: 4 (over x, core).
Axes of the slice: x: 2, y: 2, z: 4, core: 2. Of those that a mesh axis runs over, the one named last changes fastest.
Arguments:
- queries: bfloat16 [4096, 1024], P(('grp', 'seq')), may hold values from -160 to 160
- states: bfloat16 [4096, 1024], P(('grp', 'seq')), may hold values from -6 to 6
- behavior_keys: bfloat16 [8, 2048, 1024], P('grp', 'seq'), may hold values from -7 to 7
- behavior_values: bfloat16 [8, 2048, 1024], P('grp', 'seq'), may hold values from -6 to 6
- lengths: int32 [8], P('grp'), may hold values from 512 to 2048, as said below
- user_of: int32 [4096], P('grp'), may hold values from 0 to 1
- out_weight: bfloat16 [1024, 1024], replicated, may hold values from -0.1875 to 0.1875
- norm_gain: float32 [1024], replicated, may hold values from 0.1 to 1.9
- routes: int32 [4096, 2], P(('grp', 'seq')), may hold values from 0 to 31, all different within a row; in each aligned block of 256 rows (0 to 255, 256 to 511, ...) at most 16 rows name the same one
- route_weights: float32 [4096, 2], P(('grp', 'seq')), may hold values from 0.25 to 1
- expert_up: bfloat16 [32, 1024, 4096], P(('seq', 'grp')), may hold values from -0.1875 to 0.1875
- expert_down: bfloat16 [32, 4096, 1024], P(('seq', 'grp')), may hold values from -0.09375 to 0.09375
Outputs:
- block_out: bfloat16 [4096, 1024], P(('grp', 'seq'))
Inputs may be any that keep to these rules, and one draw needn't show every extreme that they name: For the tokens of one device, no expert is named by more than 16 of their routes. `lengths`: some user has all 2048 behaviors valid in every draw.
All inputs are finite; a program needn't handle non-finite values.
Results may differ from a plain program's by a relative error of at most 0.0065.
Values may be sent and summed in bfloat16 or wider, within the bound.
A program may use at most 128 MiB of HBM per device.

v0:
```python
import math

import jax
import jax.numpy as jnp
from jax import lax
from jax.sharding import PartitionSpec as P

HEADS = 8


def head_layout(rows, ratio):
    users, hist_local, width = rows.shape
    sub = hist_local // ratio
    shaped = rows.reshape(users, ratio, sub, HEADS, width // HEADS)
    return jnp.transpose(shaped, (3, 1, 0, 2, 4)).reshape(HEADS * ratio, users, sub, width // HEADS)


def attend_heads(queries, behavior_keys, behavior_values, lengths, user_of):
    seq_count = lax.axis_size("seq")
    ratio = seq_count // HEADS
    tok_count, width = queries.shape
    head_size = width // HEADS
    hist_local = behavior_keys.shape[1]
    sub = hist_local // ratio
    head = lax.axis_index("seq") // ratio
    portion = lax.axis_index("seq") % ratio
    keys_head, values_head = (
        lax.all_to_all(
            head_layout(behavior_keys, ratio), "seq", split_axis=0, concat_axis=2, tiled=True
        ),
        lax.all_to_all(
            head_layout(behavior_values, ratio), "seq", split_axis=0, concat_axis=2, tiled=True
        ),
    )
    keys_head = keys_head[0]
    values_head = values_head[0]
    spread_heads = jnp.repeat(queries.reshape(tok_count, HEADS, head_size), ratio, axis=1)
    query_send = jnp.transpose(spread_heads, (1, 0, 2))
    query_head = lax.all_to_all(query_send, "seq", split_axis=0, concat_axis=0, tiled=True).reshape(
        -1, head_size
    )
    positions = (
        jnp.arange(seq_count, dtype=jnp.int32)[:, None] * hist_local
        + portion * sub
        + jnp.arange(sub, dtype=jnp.int32)[None, :]
    ).reshape(-1)
    factor = 1.0 / math.sqrt(head_size)
    listing = []
    for member in range(keys_head.shape[0]):
        scores = (
            jnp.einsum(
                "gd,pd->gp", query_head, keys_head[member], preferred_element_type=jnp.float32
            )
            * factor
        )
        usable = (user_of == member)[:, None] & (positions < lengths[member])[None, :]
        listing.append((jnp.where(usable, scores, -1e30), usable))
    local_peak = listing[0][0].max(-1)
    for scores, usable in listing[1:]:
        local_peak = jnp.maximum(local_peak, scores.max(-1))
    columns = jnp.arange(HEADS, dtype=jnp.int32)[None, :]
    placed = jnp.where(columns == head, local_peak[:, None], -1e30)
    every_peak = lax.pmax(placed.astype(jnp.bfloat16), "seq").astype(placed.dtype)
    peaks = lax.dynamic_slice_in_dim(every_peak, head, 1, 1)[:, 0]
    numer = None
    denom = None
    for member in range(len(listing)):
        scores, usable = listing[member]
        probs = jnp.where(usable, jnp.exp(scores - peaks[:, None]), 0.0)
        term = jnp.dot(
            probs.astype(jnp.bfloat16), values_head[member], preferred_element_type=jnp.float32
        )
        if numer is None:
            numer, denom = (term, probs.sum(-1))
        else:
            numer, denom = (numer + term, denom + probs.sum(-1))
    numer_back, denom_back = (
        lax.all_to_all(
            numer.reshape(seq_count, tok_count, head_size).astype(jnp.bfloat16),
            "seq",
            split_axis=0,
            concat_axis=0,
            tiled=True,
        ).astype(jnp.float32),
        lax.all_to_all(
            denom.reshape(seq_count, tok_count, 1).astype(jnp.bfloat16),
            "seq",
            split_axis=0,
            concat_axis=0,
            tiled=True,
        ).astype(jnp.float32),
    )
    numer_own = numer_back.reshape(HEADS, ratio, tok_count, head_size).sum(1)
    denom_own = denom_back.reshape(HEADS, ratio, tok_count).sum(1)
    return (jnp.transpose(numer_own, (1, 0, 2)), jnp.transpose(denom_own, (1, 0)))


def body(
    queries,
    states,
    behavior_keys,
    behavior_values,
    lengths,
    user_of,
    out_weight,
    norm_gain,
    routes,
    route_weights,
    expert_up,
    expert_down,
):
    tok_count = queries.shape[0]
    numer, denom = attend_heads(queries, behavior_keys, behavior_values, lengths, user_of)
    attended = (numer / denom[..., None]).reshape(queries.shape).astype(jnp.bfloat16)
    residual = states.astype(jnp.float32) + jnp.dot(
        attended, out_weight, preferred_element_type=jnp.float32
    )
    spread = jnp.mean(residual * residual, axis=-1, keepdims=True)
    normed = (residual / jnp.sqrt(spread + 1e-06) * norm_gain).astype(jnp.bfloat16)
    seq_count = lax.axis_size("seq")
    grp_count = lax.axis_size("grp")
    experts_all = seq_count * grp_count
    width = normed.shape[1]
    top = routes.shape[1]
    capacity = max(2, 2 * tok_count * top // experts_all)
    flat = routes.reshape(-1)
    onehot = (flat[:, None] == jnp.arange(experts_all, dtype=jnp.int32)[None, :]).astype(jnp.int32)
    earlier = jnp.cumsum(onehot, axis=0) - onehot
    slots = jnp.sum(earlier * onehot, axis=1)
    target = flat * capacity + slots
    rows = jnp.broadcast_to(normed[:, None, :], (tok_count, top, width)).reshape(-1, width)
    buffer = jnp.zeros((experts_all * capacity, width), jnp.bfloat16).at[target].set(rows)
    sent = lax.all_to_all(
        buffer.reshape(experts_all, capacity, width),
        ("seq", "grp"),
        split_axis=0,
        concat_axis=0,
        tiled=True,
    )
    shape = sent.shape
    flat_rows = sent.reshape(-1, shape[-1])
    hidden = jax.nn.gelu(
        jnp.dot(flat_rows, expert_up[0], preferred_element_type=jnp.float32)
    ).astype(jnp.bfloat16)
    received = (
        jnp.dot(hidden, expert_down[0], preferred_element_type=jnp.float32)
        .astype(jnp.bfloat16)
        .reshape(shape)
    )
    answered = lax.all_to_all(received, ("seq", "grp"), split_axis=0, concat_axis=0, tiled=True)
    picked = answered.reshape(-1, width)[target].astype(jnp.float32).reshape(tok_count, top, width)
    mixed = jnp.sum(picked * route_weights[:, :, None], axis=1)
    return (residual + mixed).astype(jnp.bfloat16)


def solution(mesh):
    return jax.shard_map(
        body,
        mesh=mesh,
        in_specs=(
            P(("grp", "seq"), None),
            P(("grp", "seq"), None),
            P("grp", "seq", None),
            P("grp", "seq", None),
            P("grp"),
            P("grp"),
            P(),
            P(),
            P(("grp", "seq"), None),
            P(("grp", "seq"), None),
            P(("seq", "grp"), None, None),
            P(("seq", "grp"), None, None),
        ),
        out_specs=P(("grp", "seq"), None),
        check_vma=False,
    )
```

profile of v0, /device:TPU:0, one launch (start us, length us, event | category | flops | bytes accessed | tf_op | source)
XLA Modules:
  0.0 248.2 jit_solution(200376153057666010)
XLA Ops:
  2.0 7.3 %all-to-all-start = ((bf16[8,128,128]{1,2,0:T(8,128)(2,1)}), bf16[8,128,128]{1,2,0:T(8,128)(2,1)S(1)}, u32[]{:S(2)}, u32[]{:S(2)}) async-start(bf16[8,128,128]{1,2,0:T(8,128)(2,1)} %bitcast.2), calls=%async_computation | async-start | bytes 524288 | tf_op jit(solution)/shard_map/all_to_all | solution.py:39
  11.9 6.3 %all-to-all-done = bf16[8,128,128]{1,2,0:T(8,128)(2,1)S(1)} async-done(((bf16[8,128,128]{1,2,0:T(8,128)(2,1)}), bf16[8,128,128]{1,2,0:T(8,128)(2,1)S(1)}, u32[]{:S(2)}, u32[]{:S(2)}) %all-to-all-start) | async-done | bytes 262176 | tf_op jit(solution)/shard_map/all_to_all | solution.py:39
  18.2 3.6 %all-to-all-start.2 = ((bf16[8,2,256,128]{2,3,1,0:T(8,128)(2,1)}), bf16[8,2,256,128]{2,3,1,0:T(8,128)(2,1)S(1)}, u32[]{:S(2)}, u32[]{:S(2)}) async-start(bf16[8,2,256,128]{2,3,1,0:T(8,128)(2,1)} %copy.54), calls=%async_computation.2 | async-start | bytes 2097152 | tf_op jit(solution)/shard_map/all_to_all | solution.py:31
  21.8 2.3 copy.50
  24.1 2.3 copy.51
  26.4 21.0 %all-to-all-done.2 = bf16[8,2,256,128]{2,3,1,0:T(8,128)(2,1)S(1)} async-done(((bf16[8,2,256,128]{2,3,1,0:T(8,128)(2,1)}), bf16[8,2,256,128]{2,3,1,0:T(8,128)(2,1)S(1)}, u32[]{:S(2)}, u32[]{:S(2)}) %all-to-all-start.2) | async-done | bytes 1048608 | tf_op jit(solution)/shard_map/all_to_all | solution.py:31
  47.3 4.2 %all-to-all-start.1 = ((bf16[8,2,256,128]{2,3,1,0:T(8,128)(2,1)}), bf16[8,2,256,128]{2,3,1,0:T(8,128)(2,1)}, u32[]{:S(2)}, u32[]{:S(2)}) async-start(bf16[8,2,256,128]{2,3,1,0:T(8,128)(2,1)} %copy.51), calls=%async_computation.1 | async-start | bytes 2097152 | tf_op jit(solution)/shard_map/all_to_all | solution.py:28
  56.1 2.3 fusion.63
  58.3 18.7 %all-to-all-done.1 = bf16[8,2,256,128]{2,3,1,0:T(8,128)(2,1)} async-done(((bf16[8,2,256,128]{2,3,1,0:T(8,128)(2,1)}), bf16[8,2,256,128]{2,3,1,0:T(8,128)(2,1)}, u32[]{:S(2)}, u32[]{:S(2)}) %all-to-all-start.1) | async-done | bytes 1048608 | tf_op jit(solution)/shard_map/all_to_all | solution.py:28
  78.8 4.2 %fusion.13 = (bf16[1024]{0:T(1024)(128)(2,1)S(1)}, f32[1024,2048]{1,0:T(8,128)}) fusion(pred[2048]{0:T(1024)(128)(4,1)S(1)} %lt.49, pred[1024]{0:T(1024)(128)(4,1)S(1)} %get-tuple-element.11, bf16[1024,128]{1,0:T(8,128)(2,1)S(1)} %bitcast.99, bf16[2048,128]{1,0:T(8,128)(2,1)S(1)} %bitcast.98), kind=kOutput, calls=%fused_computation.20 | convolution fusion | flops 545258496 | bytes 9180160 | tf_op jit(solution)/shard_map/gd,pd->gp/dot_general | solution.py:51
  83.0 4.2 %fusion.12 = (bf16[1024]{0:T(1024)(128)(2,1)S(1)}, f32[1024,2048]{1,0:T(8,128)}) fusion(pred[2048]{0:T(1024)(128)(4,1)S(1)} %lt.46, pred[1024]{0:T(1024)(128)(4,1)S(1)} %get-tuple-element.12, bf16[1024,128]{1,0:T(8,128)(2,1)S(1)} %bitcast.100, bf16[2048,128]{1,0:T(8,128)(2,1)S(1)} %bitcast.97), kind=kOutput, calls=%fused_computation.19 | convolution fusion | flops 545258496 | bytes 9180160 | tf_op jit(solution)/shard_map/gd,pd->gp/dot_general | solution.py:51
  87.3 34.9 %pmax.7 = bf16[1024,8]{0,1:T(8,128)(2,1)S(1)} all-reduce(bf16[1024,8]{0,1:T(8,128)(2,1)S(1)} %select_convert_fusion), channel_id=1, replica_groups=mesh['seq'=8,'grp'=4] {'seq'}, use_global_device_ids=true, to_apply=%region_2.3 | all-reduce | flops 8192 | bytes 32768 | tf_op jit(solution)/shard_map/pmax | solution.py:63
  122.3 6.6 %fusion.22 = f32[1024,128]{1,0:T(8,128)} fusion(bf16[2048,128]{1,0:T(8,128)(2,1)S(1)} %bitcast.96, f32[1024,2048]{1,0:T(8,128)} %get-tuple-element.20, f32[1024]{0:T(1024)S(1)} %bitcast.102, pred[2048]{0:T(1024)(128)(4,1)S(1)} %lt.49, pred[1024]{0:T(1024)(128)(4,1)S(1)} %get-tuple-element.11), kind=kOutput, calls=%fused_computation.28 | convolution fusion | flops 549453824 | bytes 9444352 | tf_op jit(solution)/shard_map/dot_general | solution.py:70
  130.6 5.9 %fusion.16 = (f32[1024]{0:T(1024)S(1)}, f32[1024]{0:T(1024)S(1)}) fusion(f32[1024,2048]{1,0:T(8,128)S(1)} %copy-done.2, f32[1024]{0:T(1024)S(1)} %bitcast.103, pred[2048]{0:T(1024)(128)(4,1)S(1)} %lt.49, pred[1024]{0:T(1024)(128)(4,1)S(1)} %get-tuple-element.11, f32[1024,2048]{1,0:T(8,128)S(1)} %copy-done.1, pred[2048]{0:T(1024)(128)(4,1)S(1)} %lt.46, ...), kind=kLoop, calls=%fused_computation.23 | loop fusion | flops 25163776 | bytes 16795648 | tf_op jit(solution)/shard_map/reduce_sum | solution.py:76
  137.1 3.2 %all-to-all-start.4 = ((bf16[8,128,1]{1,2,0:T(2,128)(2,1)}), bf16[8,128,1]{1,2,0:T(2,128)(2,1)S(1)}, u32[]{:S(2)}, u32[]{:S(2)}) async-start(bf16[8,128,1]{1,2,0:T(2,128)(2,1)} %copy.57), calls=%async_computation.4 | async-start | bytes 8192 | tf_op jit(solution)/shard_map/all_to_all | solution.py:85
  140.3 5.8 %fusion.40 = bf16[1024,128]{1,0:T(8,128)(2,1)S(1)} fusion(f32[1024,128]{1,0:T(8,128)} %fusion.22, bf16[2048,128]{1,0:T(8,128)(2,1)S(1)} %bitcast.95, f32[1024,2048]{1,0:T(8,128)} %get-tuple-element.18, f32[1024]{0:T(1024)S(1)} %bitcast.104, pred[2048]{0:T(1024)(128)(4,1)S(1)} %lt.46, pred[1024]{0:T(1024)(128)(4,1)S(1)} %get-tuple-element.12), kind=kOutput, calls=%fused_computation.33 | convolution fusion | flops 549715968 | bytes 9706496 | tf_op jit(solution)/shard_map/dot_general | solution.py:70
  147.0 5.9 %all-to-all-start.3 = ((bf16[8,128,128]{1,2,0:T(8,128)(2,1)}), bf16[8,128,128]{1,2,0:T(8,128)(2,1)S(1)}, u32[]{:S(2)}, u32[]{:S(2)}) async-start(bf16[8,128,128]{1,2,0:T(8,128)(2,1)} %copy.56), calls=%async_computation.3 | async-start | bytes 524288 | tf_op jit(solution)/shard_map/all_to_all | solution.py:78
  154.3 6.9 %all-to-all-done.3 = bf16[8,128,128]{1,2,0:T(8,128)(2,1)S(1)} async-done(((bf16[8,128,128]{1,2,0:T(8,128)(2,1)}), bf16[8,128,128]{1,2,0:T(8,128)(2,1)S(1)}, u32[]{:S(2)}, u32[]{:S(2)}) %all-to-all-start.3) | async-done | bytes 262176 | tf_op jit(solution)/shard_map/all_to_all | solution.py:78
  164.0 2.4 scatter_custom_fusion
  166.4 29.0 %all_to_all.55 = bf16[32,16,1024]{2,1,0:T(8,128)(2,1)} all-to-all(bf16[32,16,1024]{2,1,0:T(8,128)(2,1)S(1)} %bitcast.89), channel_id=1, replica_groups=mesh['seq'=8,'grp'=4] {'seq','grp'}, dimensions={0} | all-to-all | bytes 2097152 | tf_op jit(solution)/shard_map/all_to_all | solution.py:133
  195.5 16.1 %fusion.30 = bf16[512,1024]{1,0:T(8,128)(2,1)} fusion(bf16[1,4096,1024]{2,1,0:T(8,128)(2,1)} %param.23, bf16[512,1024]{1,0:T(8,128)(2,1)} %bitcast.93, bf16[1,1024,4096]{2,1,0:T(8,128)(2,1)} %param.22), kind=kOutput, calls=%fused_computation.30 | convolution fusion | flops 8609333248 | bytes 18874368 | tf_op jit(solution)/shard_map/dot_general | solution.py:146
  211.5 3.8 %all-to-all-start.6 = ((bf16[32,16,1024]{2,1,0:T(8,128)(2,1)}), bf16[32,16,1024]{2,1,0:T(8,128)(2,1)S(1)}, u32[]{:S(2)}, u32[]{:S(2)}) async-start(bf16[32,16,1024]{2,1,0:T(8,128)(2,1)} %bitcast.92), calls=%async_computation.6 | async-start | bytes 2097152 | tf_op jit(solution)/shard_map/all_to_all | solution.py:150
  215.5 25.9 %all-to-all-done.6 = bf16[32,16,1024]{2,1,0:T(8,128)(2,1)S(1)} async-done(((bf16[32,16,1024]{2,1,0:T(8,128)(2,1)}), bf16[32,16,1024]{2,1,0:T(8,128)(2,1)S(1)}, u32[]{:S(2)}, u32[]{:S(2)}) %all-to-all-start.6) | async-done | bytes 1048608 | tf_op jit(solution)/shard_map/all_to_all | solution.py:150
  241.3 2.0 gather_fusion
  (72 shorter events, 23.0 us)
Async XLA Ops:
  0.0 161.2 %copy-start = (bf16[1024,1024]{1,0:T(8,128)(2,1)S(1)}, bf16[1024,1024]{1,0:T(8,128)(2,1)}, u32[]{:S(2)}) copy-start(bf16[1024,1024]{1,0:T(8,128)(2,1)} %param.18) | copy-start | bytes 6291460
  0.0 51.6 %copy-start.11 = (s32[2]{0:T(128)S(1)}, s32[2]{0:T(128)}, u32[]{:S(2)}) copy-start(s32[2]{0:T(128)} %param.16) | copy-start | bytes 28
  0.0 53.6 %copy-start.9 = (s32[128,2]{0,1:T(2,128)S(1)}, s32[128,2]{0,1:T(2,128)}, u32[]{:S(2)}) copy-start(s32[128,2]{0,1:T(2,128)} %param.20) | copy-start | bytes 3076
  0.0 53.8 %copy-start.10 = (s32[1024]{0:T(1024)S(1)}, s32[1024]{0:T(1024)}, u32[]{:S(2)}) copy-start(s32[1024]{0:T(1024)} %param.17) | copy-start | bytes 12292
  2.0 16.2 %all-to-all-start = ((bf16[8,128,128]{1,2,0:T(8,128)(2,1)}), bf16[8,128,128]{1,2,0:T(8,128)(2,1)S(1)}, u32[]{:S(2)}, u32[]{:S(2)}) async-start(bf16[8,128,128]{1,2,0:T(8,128)(2,1)} %bitcast.2), calls=%async_computation | async-start | bytes 524288 | tf_op jit(solution)/shard_map/all_to_all | solution.py:39
  18.2 29.2 %all-to-all-start.2 = ((bf16[8,2,256,128]{2,3,1,0:T(8,128)(2,1)}), bf16[8,2,256,128]{2,3,1,0:T(8,128)(2,1)S(1)}, u32[]{:S(2)}, u32[]{:S(2)}) async-start(bf16[8,2,256,128]{2,3,1,0:T(8,128)(2,1)} %copy.54), calls=%async_computation.2 | async-start | bytes 2097152 | tf_op jit(solution)/shard_map/all_to_all | solution.py:31
  47.3 29.7 %all-to-all-start.1 = ((bf16[8,2,256,128]{2,3,1,0:T(8,128)(2,1)}), bf16[8,2,256,128]{2,3,1,0:T(8,128)(2,1)}, u32[]{:S(2)}, u32[]{:S(2)}) async-start(bf16[8,2,256,128]{2,3,1,0:T(8,128)(2,1)} %copy.51), calls=%async_computation.1 | async-start | bytes 2097152 | tf_op jit(solution)/shard_map/all_to_all | solution.py:28
  54.7 24.0 %copy-start.6 = (bf16[8,128,128]{2,1,0:T(8,128)(2,1)S(1)}, bf16[8,128,128]{2,1,0:T(8,128)(2,1)}, u32[]{:S(2)}) copy-start(bf16[8,128,128]{2,1,0:T(8,128)(2,1)} %copy.49) | copy-start | bytes 786436
  83.0 39.2 %copy-start.5 = (bf16[1,1,8,256,128]{4,3,2,1,0:T(8,128)(2,1)S(1)}, bf16[1,1,8,256,128]{4,3,2,1,0:T(8,128)(2,1)}, u32[]{:S(2)}) copy-start(bf16[1,1,8,256,128]{4,3,2,1,0:T(8,128)(2,1)} %get-tuple-element.8) | copy-start | bytes 1572868
  122.2 6.6 %copy-start.1 = (f32[1024,2048]{1,0:T(8,128)S(1)}, f32[1024,2048]{1,0:T(8,128)}, u32[]{:S(2)}) copy-start(f32[1024,2048]{1,0:T(8,128)} %get-tuple-element.18) | copy-start | bytes 25165828
  122.3 8.3 %copy-start.2 = (f32[1024,2048]{1,0:T(8,128)S(1)}, f32[1024,2048]{1,0:T(8,128)}, u32[]{:S(2)}) copy-start(f32[1024,2048]{1,0:T(8,128)} %get-tuple-element.20) | copy-start | bytes 25165828
  130.6 9.7 %copy-start.4 = (bf16[1,1,8,256,128]{4,3,2,1,0:T(8,128)(2,1)S(1)}, bf16[1,1,8,256,128]{4,3,2,1,0:T(8,128)(2,1)}, u32[]{:S(2)}) copy-start(bf16[1,1,8,256,128]{4,3,2,1,0:T(8,128)(2,1)} %get-tuple-element.7) | copy-start | bytes 1572868
  137.1 9.9 %all-to-all-start.4 = ((bf16[8,128,1]{1,2,0:T(2,128)(2,1)}), bf16[8,128,1]{1,2,0:T(2,128)(2,1)S(1)}, u32[]{:S(2)}, u32[]{:S(2)}) async-start(bf16[8,128,1]{1,2,0:T(2,128)(2,1)} %copy.57), calls=%async_computation.4 | async-start | bytes 8192 | tf_op jit(solution)/shard_map/all_to_all | solution.py:85
  140.3 20.9 %copy-start.7 = (bf16[128,1024]{1,0:T(8,128)(2,1)S(1)}, bf16[128,1024]{1,0:T(8,128)(2,1)}, u32[]{:S(2)}) copy-start(bf16[128,1024]{1,0:T(8,128)(2,1)} %param.13) | copy-start | bytes 786436
  140.3 22.3 %copy-start.8 = (f32[1024]{0:T(1024)S(1)}, f32[1024]{0:T(1024)}, u32[]{:S(2)}) copy-start(f32[1024]{0:T(1024)} %param.19) | copy-start | bytes 12292
  147.0 14.1 %all-to-all-start.3 = ((bf16[8,128,128]{1,2,0:T(8,128)(2,1)}), bf16[8,128,128]{1,2,0:T(8,128)(2,1)S(1)}, u32[]{:S(2)}, u32[]{:S(2)}) async-start(bf16[8,128,128]{1,2,0:T(8,128)(2,1)} %copy.56), calls=%async_computation.3 | async-start | bytes 524288 | tf_op jit(solution)/shard_map/all_to_all | solution.py:78
  161.8 0.8 copy-start.3
  195.5 19.9 %copy-start.12 = (f32[128,2]{0,1:T(2,128)S(1)}, f32[128,2]{0,1:T(2,128)}, u32[]{:S(2)}) copy-start(f32[128,2]{0,1:T(2,128)} %param.21) | copy-start | bytes 3076
  211.5 29.8 %all-to-all-start.6 = ((bf16[32,16,1024]{2,1,0:T(8,128)(2,1)}), bf16[32,16,1024]{2,1,0:T(8,128)(2,1)S(1)}, u32[]{:S(2)}, u32[]{:S(2)}) async-start(bf16[32,16,1024]{2,1,0:T(8,128)(2,1)} %bitcast.92), calls=%async_computation.6 | async-start | bytes 2097152 | tf_op jit(solution)/shard_map/all_to_all | solution.py:150
where the time goes:
time: 249 us; the launch traced here: 248 us
  waiting for transfers between devices  78.7 us (32%)
  blocking collectives  64 us (26%)
  matrix products  37.4 us (15%)
  local copies, waits for them, and re-layouts  28.1 us (11%)
  starting transfers between devices  28.1 us (11%)
  other arithmetic  11.4 us (5%)
    pmax x1, blocking collectives, attend_heads(): lax.pmax(placed.astype(jnp.bfloat16), 'seq').astype(placed.dtype)  34.9 us
    all_to_all x1, blocking collectives, body(): lax.all_to_all(buffer.reshape(experts_all, capacity, width), ('seq', 'grp...  29 us
    all_to_all x1, waiting for transfers between devices, body(): lax.all_to_all(received, ('seq', 'grp'), split_axis=0, concat_axis=0, til...  25.9 us
    all_to_all x1, waiting for transfers between devices, attend_heads(): lax.all_to_all(head_layout(behavior_values, ratio), 'seq', split_axis=0,...  21 us
    all_to_all x1, waiting for transfers between devices, attend_heads(): lax.all_to_all(head_layout(behavior_keys, ratio), 'seq', split_axis=0, co...  18.7 us
    dot_general x1, matrix products, body(): jnp.dot(hidden, expert_down[0], preferred_element_type=jnp.float32)  16.1 us
    dot_general x2, matrix products, attend_heads(): jnp.dot(probs.astype(jnp.bfloat16), values_head[member], preferred_elemen...  12.4 us
    unnamed x31, local copies, waits for them, and re-layouts  8.49 us
  transfers between devices with their start and end apart: 6, of which 5 were waited for; matrix products, arithmetic and copies ran while one was open for 9% of the time, Pallas kernels for 0%

commit v1 on v0

--- a/solution.py
+++ b/solution.py
@@ -55,44 +55,36 @@
         )
         usable = (user_of == member)[:, None] & (positions < lengths[member])[None, :]
         listing.append((jnp.where(usable, scores, -1e30), usable))
-    local_peak = listing[0][0].max(-1)
+    peak = listing[0][0].max(-1, keepdims=True)
     for scores, usable in listing[1:]:
-        local_peak = jnp.maximum(local_peak, scores.max(-1))
-    columns = jnp.arange(HEADS, dtype=jnp.int32)[None, :]
-    placed = jnp.where(columns == head, local_peak[:, None], -1e30)
-    every_peak = lax.pmax(placed.astype(jnp.bfloat16), "seq").astype(placed.dtype)
-    peaks = lax.dynamic_slice_in_dim(every_peak, head, 1, 1)[:, 0]
+        peak = jnp.maximum(peak, scores.max(-1, keepdims=True))
     numer = None
     denom = None
     for member in range(len(listing)):
         scores, usable = listing[member]
-        probs = jnp.where(usable, jnp.exp(scores - peaks[:, None]), 0.0)
+        probs = jnp.where(usable, jnp.exp(scores - peak), 0.0)
         term = jnp.dot(
             probs.astype(jnp.bfloat16), values_head[member], preferred_element_type=jnp.float32
         )
-        if numer is None:
-            numer, denom = (term, probs.sum(-1))
-        else:
-            numer, denom = (numer + term, denom + probs.sum(-1))
-    numer_back, denom_back = (
-        lax.all_to_all(
-            numer.reshape(seq_count, tok_count, head_size).astype(jnp.bfloat16),
-            "seq",
-            split_axis=0,
-            concat_axis=0,
-            tiled=True,
-        ).astype(jnp.float32),
-        lax.all_to_all(
-            denom.reshape(seq_count, tok_count, 1).astype(jnp.bfloat16),
-            "seq",
-            split_axis=0,
-            concat_axis=0,
-            tiled=True,
-        ).astype(jnp.float32),
+        total = probs.sum(-1, keepdims=True)
+        numer, denom = (term, total) if numer is None else (numer + term, denom + total)
+    if ratio == 1:
+        part = (numer / denom).astype(jnp.bfloat16)
+    else:
+        part = (numer / jnp.maximum(denom, 1e-30)).astype(jnp.bfloat16)
+    part = lax.all_to_all(
+        part.reshape(seq_count, tok_count, head_size), "seq", split_axis=0, concat_axis=0, tiled=True
     )
-    numer_own = numer_back.reshape(HEADS, ratio, tok_count, head_size).sum(1)
-    denom_own = denom_back.reshape(HEADS, ratio, tok_count).sum(1)
-    return (jnp.transpose(numer_own, (1, 0, 2)), jnp.transpose(denom_own, (1, 0)))
+    if ratio == 1:
+        return jnp.transpose(part, (1, 0, 2)).reshape(tok_count, width)
+    level = jnp.where(denom > 0, peak + jnp.log(jnp.maximum(denom, 1e-30)), -1e30)
+    level = lax.all_to_all(
+        level.reshape(seq_count, tok_count, 1), "seq", split_axis=0, concat_axis=0, tiled=True
+    ).reshape(HEADS, ratio, tok_count, 1)
+    share = jax.nn.softmax(level, axis=1)
+    part = part.reshape(HEADS, ratio, tok_count, head_size).astype(jnp.float32)
+    joined = (part * share).sum(1)
+    return jnp.transpose(joined, (1, 0, 2)).reshape(tok_count, width).astype(jnp.bfloat16)
 
 
 def body(
@@ -110,8 +102,7 @@
     expert_down,
 ):
     tok_count = queries.shape[0]
-    numer, denom = attend_heads(queries, behavior_keys, behavior_values, lengths, user_of)
-    attended = (numer / denom[..., None]).reshape(queries.shape).astype(jnp.bfloat16)
+    attended = attend_heads(queries, behavior_keys, behavior_values, lengths, user_of)
     residual = states.astype(jnp.float32) + jnp.dot(
         attended, out_weight, preferred_element_type=jnp.float32
     )

time: 249 us -> 196 us (0.79)
  blocking collectives: 64 us -> 29.7 us
  matrix products: 37.4 us -> 26 us
  starting transfers between devices: 28.1 us -> 22.6 us
    pmax x1 -> x0, blocking collectives: 34.9 us -> none  [attend_heads(): lax.pmax(placed.astype(jnp.bfloat16), 'seq').astype(placed.dtype)]
    dot_general x2, matrix products: 12.4 us -> 5.37 us  [attend_heads(): jnp.dot(probs.astype(jnp.bfloat16), values_head[member], preferred_elemen...]
    all_to_all x2 -> x1, starting transfers between devices: 9.15 us -> 3.59 us  [attend_heads(): lax.all_to_all(part.reshape(seq_count, tok_count, head_size), 'seq', spli...]
    dot_general x2, matrix products: 8.42 us -> 4.01 us  [attend_heads(): jnp.einsum('gd,pd->gp', query_head, keys_head[member], preferred_element_...]
    unnamed x31 -> x27, local copies, waits for them, and re-layouts: 8.49 us -> 6.74 us
    all_to_all x2 -> x1, waiting for transfers between devices: 6.87 us -> 7.52 us  [attend_heads(): lax.all_to_all(part.reshape(seq_count, tok_count, head_size), 'seq', spli...]
  transfers between devices with their start and end apart: 6 -> 5, of which waited for: 5 -> 5; matrix products, arithmetic and copies ran while one was open for 9% -> 8% of each run, Pallas kernels for 0% -> 0%
where the time goes in v1:
time: 196 us; the launch traced here: 195 us
  waiting for transfers between devices  79.4 us (41%)
  blocking collectives  29.7 us (15%)
  matrix products  26 us (13%)
  local copies, waits for them, and re-layouts  25.8 us (13%)
  starting transfers between devices  22.6 us (12%)
  other arithmetic  11.3 us (6%)
    all_to_all x1, blocking collectives, body(): lax.all_to_all(buffer.reshape(experts_all, capacity, width), ('seq', 'grp...  29.7 us
    all_to_all x1, waiting for transfers between devices, body(): lax.all_to_all(received, ('seq', 'grp'), split_axis=0, concat_axis=0, til...  25.9 us
    all_to_all x1, waiting for transfers between devices, attend_heads(): lax.all_to_all(head_layout(behavior_values, ratio), 'seq', split_axis=0,...  21 us
    all_to_all x1, waiting for transfers between devices, attend_heads(): lax.all_to_all(head_layout(behavior_keys, ratio), 'seq', split_axis=0, co...  18.7 us
    dot_general x1, matrix products, body(): jnp.dot(hidden, expert_down[0], preferred_element_type=jnp.float32)  16.1 us
    all_to_all x1, waiting for transfers between devices, attend_heads(): lax.all_to_all(part.reshape(seq_count, tok_count, head_size), 'seq', spli...  7.52 us
    all_to_all x1, starting transfers between devices, attend_heads(): lax.all_to_all(query_send, 'seq', split_axis=0, concat_axis=0, tiled=True)  7.32 us
    unnamed x27, local copies, waits for them, and re-layouts  6.74 us
  transfers between devices with their start and end apart: 5, of which 5 were waited for; matrix products, arithmetic and copies ran while one was open for 8% of the time, Pallas kernels for 0%

profile of v1, /device:TPU:0, one launch (start us, length us, event | category | flops | bytes accessed | tf_op | source)
XLA Modules:
  0.0 195.1 jit_solution(6868873436569652747)
XLA Ops:
  0.0 1.9 copy.34
  2.0 7.3 %all-to-all-start = ((bf16[8,128,128]{1,2,0:T(8,128)(2,1)}), bf16[8,128,128]{1,2,0:T(8,128)(2,1)S(1)}, u32[]{:S(2)}, u32[]{:S(2)}) async-start(bf16[8,128,128]{1,2,0:T(8,128)(2,1)} %bitcast.2), calls=%async_computation | async-start | bytes 524288 | tf_op jit(solution)/shard_map/all_to_all | solution.py:39
  11.9 6.3 %all-to-all-done = bf16[8,128,128]{1,2,0:T(8,128)(2,1)S(1)} async-done(((bf16[8,128,128]{1,2,0:T(8,128)(2,1)}), bf16[8,128,128]{1,2,0:T(8,128)(2,1)S(1)}, u32[]{:S(2)}, u32[]{:S(2)}) %all-to-all-start) | async-done | bytes 262176 | tf_op jit(solution)/shard_map/all_to_all | solution.py:39
  18.2 3.6 %all-to-all-start.2 = ((bf16[8,2,256,128]{2,3,1,0:T(8,128)(2,1)}), bf16[8,2,256,128]{2,3,1,0:T(8,128)(2,1)S(1)}, u32[]{:S(2)}, u32[]{:S(2)}) async-start(bf16[8,2,256,128]{2,3,1,0:T(8,128)(2,1)} %copy.40), calls=%async_computation.2 | async-start | bytes 2097152 | tf_op jit(solution)/shard_map/all_to_all | solution.py:31
  21.8 2.3 %copy.36 = bf16[2,256,1024]{1,2,0:T(8,128)(2,1)} copy(bf16[2,256,1024]{2,1,0:T(8,128)(2,1)} %param.14) | data formatting | bytes 2097152 | tf_op args[2]
  24.1 2.3 %copy.37 = bf16[8,2,256,128]{2,3,1,0:T(8,128)(2,1)} copy(bf16[8,2,256,128]{2,3,0,1:T(8,128)(2,1)} %bitcast.83) | data formatting | bytes 2097152 | tf_op jit(solution)/shard_map/reshape | solution.py:15
  26.4 21.0 %all-to-all-done.2 = bf16[8,2,256,128]{2,3,1,0:T(8,128)(2,1)S(1)} async-done(((bf16[8,2,256,128]{2,3,1,0:T(8,128)(2,1)}), bf16[8,2,256,128]{2,3,1,0:T(8,128)(2,1)S(1)}, u32[]{:S(2)}, u32[]{:S(2)}) %all-to-all-start.2) | async-done | bytes 1048608 | tf_op jit(solution)/shard_map/all_to_all | solution.py:31
  47.3 4.2 %all-to-all-start.1 = ((bf16[8,2,256,128]{2,3,1,0:T(8,128)(2,1)}), bf16[8,2,256,128]{2,3,1,0:T(8,128)(2,1)}, u32[]{:S(2)}, u32[]{:S(2)}) async-start(bf16[8,2,256,128]{2,3,1,0:T(8,128)(2,1)} %copy.37), calls=%async_computation.1 | async-start | bytes 2097152 | tf_op jit(solution)/shard_map/all_to_all | solution.py:28
  56.0 2.3 %fusion.64 = (bf16[1,1,8,256,128]{4,3,2,1,0:T(8,128)(2,1)}, bf16[1,1,8,256,128]{4,3,2,1,0:T(8,128)(2,1)}) fusion(bf16[1,2,8,256,128]{4,3,2,1,0:T(8,128)(2,1)} %bitcast.79), kind=kLoop, calls=%fused_computation.70 | loop fusion | bytes 2097152 | tf_op jit(solution)/shard_map/slice | solution.py:67
  58.3 18.7 %all-to-all-done.1 = bf16[8,2,256,128]{2,3,1,0:T(8,128)(2,1)} async-done(((bf16[8,2,256,128]{2,3,1,0:T(8,128)(2,1)}), bf16[8,2,256,128]{2,3,1,0:T(8,128)(2,1)}, u32[]{:S(2)}, u32[]{:S(2)}) %all-to-all-start.1) | async-done | bytes 1048608 | tf_op jit(solution)/shard_map/all_to_all | solution.py:28
  78.8 2.0 %fusion.13 = (f32[1024]{0:T(1024)S(1)}, f32[1024,2048]{1,0:T(8,128)S(1)}) fusion(pred[2048]{0:T(1024)(128)(4,1)S(1)} %lt.46, pred[1024]{0:T(1024)(128)(4,1)S(1)} %get-tuple-element.11, bf16[1024,128]{1,0:T(8,128)(2,1)S(1)} %bitcast.91, bf16[2048,128]{1,0:T(8,128)(2,1)S(1)} %bitcast.90), kind=kOutput, calls=%fused_computation.20 | convolution fusion | flops 545258496 | bytes 9182208 | tf_op jit(solution)/shard_map/gd,pd->gp/dot_general | solution.py:51
  80.8 2.0 %fusion.12 = (f32[1024]{0:T(1024)S(1)}, f32[1024,2048]{1,0:T(8,128)S(1)}) fusion(pred[2048]{0:T(1024)(128)(4,1)S(1)} %lt.43, pred[1024]{0:T(1024)(128)(4,1)S(1)} %get-tuple-element.12, bf16[1024,128]{1,0:T(8,128)(2,1)S(1)} %bitcast.92, bf16[2048,128]{1,0:T(8,128)(2,1)S(1)} %bitcast.89), kind=kOutput, calls=%fused_computation.19 | convolution fusion | flops 545258496 | bytes 9182208 | tf_op jit(solution)/shard_map/gd,pd->gp/dot_general | solution.py:51
  82.8 2.3 %fusion.22 = f32[1024,128]{1,0:T(8,128)S(1)} fusion(bf16[2048,128]{1,0:T(8,128)(2,1)S(1)} %bitcast.88, f32[1024,2048]{1,0:T(8,128)S(1)} %get-tuple-element.20, f32[1024]{0:T(1024)S(1)} %max.8, pred[2048]{0:T(1024)(128)(4,1)S(1)} %lt.46, pred[1024]{0:T(1024)(128)(4,1)S(1)} %get-tuple-element.11), kind=kOutput, calls=%fused_computation.28 | convolution fusion | flops 549453824 | bytes 9444352 | tf_op jit(solution)/shard_map/dot_general | solution.py:66
  85.2 5.9 %fusion.16 = (f32[1024]{0:T(1024)S(1)}, f32[1024]{0:T(1024)S(1)}) fusion(f32[1024,2048]{1,0:T(8,128)S(1)} %get-tuple-element.20, f32[1024]{0:T(1024)S(1)} %max.8, pred[2048]{0:T(1024)(128)(4,1)S(1)} %lt.46, pred[1024]{0:T(1024)(128)(4,1)S(1)} %get-tuple-element.11, f32[1024,2048]{1,0:T(8,128)S(1)} %get-tuple-element.18, pred[2048]{0:T(1024)(128)(4,1)S(1)} %lt.43, ...), kind=kLoop, calls=%fused_computation.23 | loop fusion | flops 25163776 | bytes 16795648 | tf_op jit(solution)/shard_map/reduce_sum | solution.py:69
  91.1 3.0 %fusion.43 = bf16[1024,128]{1,0:T(8,128)(2,1)S(1)} fusion(f32[1024,128]{1,0:T(8,128)S(1)} %fusion.22, bf16[2048,128]{1,0:T(8,128)(2,1)S(1)} %bitcast.87, f32[1024,2048]{1,0:T(8,128)S(1)} %get-tuple-element.18, f32[1024]{0:T(1024)S(1)} %max.8, pred[2048]{0:T(1024)(128)(4,1)S(1)} %lt.43, pred[1024]{0:T(1024)(128)(4,1)S(1)} %get-tuple-element.12, ...), kind=kOutput, calls=%fused_computation.35 | convolution fusion | flops 549847040 | bytes 9710592 | tf_op jit(solution)/shard_map/dot_general | solution.py:66
  95.0 3.6 %all-to-all-start.3 = ((bf16[8,128,128]{1,2,0:T(8,128)(2,1)}), bf16[8,128,128]{1,2,0:T(8,128)(2,1)S(1)}, u32[]{:S(2)}, u32[]{:S(2)}) async-start(bf16[8,128,128]{1,2,0:T(8,128)(2,1)} %copy.42), calls=%async_computation.3 | async-start | bytes 524288 | tf_op jit(solution)/shard_map/all_to_all | solution.py:75
  99.9 7.5 %all-to-all-done.3 = bf16[8,128,128]{1,2,0:T(8,128)(2,1)S(1)} async-done(((bf16[8,128,128]{1,2,0:T(8,128)(2,1)}), bf16[8,128,128]{1,2,0:T(8,128)(2,1)S(1)}, u32[]{:S(2)}, u32[]{:S(2)}) %all-to-all-start.3) | async-done | bytes 262176 | tf_op jit(solution)/shard_map/all_to_all | solution.py:75
  110.2 2.4 %scatter_custom_fusion = bf16[512,1024]{1,0:T(8,128)(2,1)S(1)} fusion(s32[256]{0:T(256)S(1)} %bitcast.94, bf16[256,1024]{1,0:T(8,128)(2,1)} %reshape.178, bf16[]{:T(256)} %constant.23.clone.1), kind=kCustom, calls=%fused_computation.39 | custom fusion | bytes 1049088 | tf_op jit(solution)/shard_map/scatter | solution.py:123
  112.7 29.7 %all_to_all.50 = bf16[32,16,1024]{2,1,0:T(8,128)(2,1)} all-to-all(bf16[32,16,1024]{2,1,0:T(8,128)(2,1)S(1)} %bitcast.81), channel_id=1, replica_groups=mesh['seq'=8,'grp'=4] {'seq','grp'}, dimensions={0} | all-to-all | bytes 2097152 | tf_op jit(solution)/shard_map/all_to_all | solution.py:124
  142.4 16.1 %fusion.30 = bf16[512,1024]{1,0:T(8,128)(2,1)} fusion(bf16[1,4096,1024]{2,1,0:T(8,128)(2,1)} %param.23, bf16[512,1024]{1,0:T(8,128)(2,1)} %bitcast.85, bf16[1,1024,4096]{2,1,0:T(8,128)(2,1)} %param.22), kind=kOutput, calls=%fused_computation.30 | convolution fusion | flops 8609333248 | bytes 18874368 | tf_op jit(solution)/shard_map/dot_general | solution.py:137
  158.4 3.8 %all-to-all-start.5 = ((bf16[32,16,1024]{2,1,0:T(8,128)(2,1)}), bf16[32,16,1024]{2,1,0:T(8,128)(2,1)S(1)}, u32[]{:S(2)}, u32[]{:S(2)}) async-start(bf16[32,16,1024]{2,1,0:T(8,128)(2,1)} %bitcast.84), calls=%async_computation.5 | async-start | bytes 2097152 | tf_op jit(solution)/shard_map/all_to_all | solution.py:141
  162.4 25.9 %all-to-all-done.5 = bf16[32,16,1024]{2,1,0:T(8,128)(2,1)S(1)} async-done(((bf16[32,16,1024]{2,1,0:T(8,128)(2,1)}), bf16[32,16,1024]{2,1,0:T(8,128)(2,1)S(1)}, u32[]{:S(2)}, u32[]{:S(2)}) %all-to-all-start.5) | async-done | bytes 1048608 | tf_op jit(solution)/shard_map/all_to_all | solution.py:141
  188.3 2.0 %gather_fusion = bf16[256,1024]{1,0:T(8,128)(2,1)} fusion(bf16[512,1024]{1,0:T(8,128)(2,1)S(1)} %bitcast.78, s32[1024]{0:T(1024)S(1)} %pad_clamp_fusion), kind=kCustom, calls=%fused_computation | custom fusion | bytes 1049600 | tf_op jit(solution)/shard_map/gather | solution.py:142
  193.3 1.8 add_convert_fusion
  (59 shorter events, 16.8 us)
Async XLA Ops:
  0.0 107.5 %copy-start = (bf16[1024,1024]{1,0:T(8,128)(2,1)S(1)}, bf16[1024,1024]{1,0:T(8,128)(2,1)}, u32[]{:S(2)}) copy-start(bf16[1024,1024]{1,0:T(8,128)(2,1)} %param.18) | copy-start | bytes 6291460
  0.0 51.6 %copy-start.9 = (s32[2]{0:T(128)S(1)}, s32[2]{0:T(128)}, u32[]{:S(2)}) copy-start(s32[2]{0:T(128)} %param.16) | copy-start | bytes 28
  0.0 53.6 %copy-start.7 = (s32[128,2]{0,1:T(2,128)S(1)}, s32[128,2]{0,1:T(2,128)}, u32[]{:S(2)}) copy-start(s32[128,2]{0,1:T(2,128)} %param.20) | copy-start | bytes 3076
  0.0 53.8 %copy-start.8 = (s32[1024]{0:T(1024)S(1)}, s32[1024]{0:T(1024)}, u32[]{:S(2)}) copy-start(s32[1024]{0:T(1024)} %param.17) | copy-start | bytes 12292
  2.0 16.2 %all-to-all-start = ((bf16[8,128,128]{1,2,0:T(8,128)(2,1)}), bf16[8,128,128]{1,2,0:T(8,128)(2,1)S(1)}, u32[]{:S(2)}, u32[]{:S(2)}) async-start(bf16[8,128,128]{1,2,0:T(8,128)(2,1)} %bitcast.2), calls=%async_computation | async-start | bytes 524288 | tf_op jit(solution)/shard_map/all_to_all | solution.py:39
  18.2 29.2 %all-to-all-start.2 = ((bf16[8,2,256,128]{2,3,1,0:T(8,128)(2,1)}), bf16[8,2,256,128]{2,3,1,0:T(8,128)(2,1)S(1)}, u32[]{:S(2)}, u32[]{:S(2)}) async-start(bf16[8,2,256,128]{2,3,1,0:T(8,128)(2,1)} %copy.40), calls=%async_computation.2 | async-start | bytes 2097152 | tf_op jit(solution)/shard_map/all_to_all | solution.py:31
  47.3 29.7 %all-to-all-start.1 = ((bf16[8,2,256,128]{2,3,1,0:T(8,128)(2,1)}), bf16[8,2,256,128]{2,3,1,0:T(8,128)(2,1)}, u32[]{:S(2)}, u32[]{:S(2)}) async-start(bf16[8,2,256,128]{2,3,1,0:T(8,128)(2,1)} %copy.37), calls=%async_computation.1 | async-start | bytes 2097152 | tf_op jit(solution)/shard_map/all_to_all | solution.py:28
  54.7 24.1 %copy-start.4 = (bf16[8,128,128]{2,1,0:T(8,128)(2,1)S(1)}, bf16[8,128,128]{2,1,0:T(8,128)(2,1)}, u32[]{:S(2)}) copy-start(bf16[8,128,128]{2,1,0:T(8,128)(2,1)} %copy.35) | copy-start | bytes 786436
  80.8 2.0 %copy-start.3 = (bf16[1,1,8,256,128]{4,3,2,1,0:T(8,128)(2,1)S(1)}, bf16[1,1,8,256,128]{4,3,2,1,0:T(8,128)(2,1)}, u32[]{:S(2)}) copy-start(bf16[1,1,8,256,128]{4,3,2,1,0:T(8,128)(2,1)} %get-tuple-element.8) | copy-start | bytes 1572868
  85.2 5.9 %copy-start.2 = (bf16[1,1,8,256,128]{4,3,2,1,0:T(8,128)(2,1)S(1)}, bf16[1,1,8,256,128]{4,3,2,1,0:T(8,128)(2,1)}, u32[]{:S(2)}) copy-start(bf16[1,1,8,256,128]{4,3,2,1,0:T(8,128)(2,1)} %get-tuple-element.7) | copy-start | bytes 1572868
  91.1 16.4 %copy-start.5 = (bf16[128,1024]{1,0:T(8,128)(2,1)S(1)}, bf16[128,1024]{1,0:T(8,128)(2,1)}, u32[]{:S(2)}) copy-start(bf16[128,1024]{1,0:T(8,128)(2,1)} %param.13) | copy-start | bytes 786436
  91.1 17.7 %copy-start.6 = (f32[1024]{0:T(1024)S(1)}, f32[1024]{0:T(1024)}, u32[]{:S(2)}) copy-start(f32[1024]{0:T(1024)} %param.19) | copy-start | bytes 12292
  95.0 12.5 %all-to-all-start.3 = ((bf16[8,128,128]{1,2,0:T(8,128)(2,1)}), bf16[8,128,128]{1,2,0:T(8,128)(2,1)S(1)}, u32[]{:S(2)}, u32[]{:S(2)}) async-start(bf16[8,128,128]{1,2,0:T(8,128)(2,1)} %copy.42), calls=%async_computation.3 | async-start | bytes 524288 | tf_op jit(solution)/shard_map/all_to_all | solution.py:75
  108.0 0.8 copy-start.1
  142.4 19.9 %copy-start.10 = (f32[128,2]{0,1:T(2,128)S(1)}, f32[128,2]{0,1:T(2,128)}, u32[]{:S(2)}) copy-start(f32[128,2]{0,1:T(2,128)} %param.21) | copy-start | bytes 3076
  158.4 29.8 %all-to-all-start.5 = ((bf16[32,16,1024]{2,1,0:T(8,128)(2,1)}), bf16[32,16,1024]{2,1,0:T(8,128)(2,1)S(1)}, u32[]{:S(2)}, u32[]{:S(2)}) async-start(bf16[32,16,1024]{2,1,0:T(8,128)(2,1)} %bitcast.84), calls=%async_computation.5 | async-start | bytes 2097152 | tf_op jit(solution)/shard_map/all_to_all | solution.py:141

commit v2 on v1

--- a/solution.py
+++ b/solution.py
@@ -1,11 +1,15 @@
+import functools
 import math
 
 import jax
 import jax.numpy as jnp
 from jax import lax
+from jax.experimental import pallas as pl
+from jax.experimental.pallas import tpu as pltpu
 from jax.sharding import PartitionSpec as P
 
 HEADS = 8
+MESH = pl.DeviceIdType.MESH
 
 
 def head_layout(rows, ratio):
@@ -87,6 +91,415 @@
     return jnp.transpose(joined, (1, 0, 2)).reshape(tok_count, width).astype(jnp.bfloat16)
 
 
+def mega_kernel(
+    seq_count,
+    grp_count,
+    cap,
+    lengths_ref,
+    q_ref,
+    k_ref,
+    v_ref,
+    up_ref,
+    down_ref,
+    wo_ref,
+    user_ref,
+    states_ref,
+    gain_ref,
+    rcol_ref,
+    rrow_ref,
+    rw_ref,
+    out_ref,
+    qbuf,
+    kbuf,
+    vbuf,
+    sbuf,
+    pbuf,
+    mbuf,
+    lbuf,
+    acc,
+    osend,
+    att,
+    res,
+    wo_v,
+    up_v,
+    down_v,
+    dsend,
+    drecv,
+    rsend,
+    ans,
+    facc,
+    wsem,
+    lsem,
+    qs,
+    qr,
+    ks,
+    kr,
+    vs,
+    vr,
+    os_,
+    or_,
+    ds_,
+    dr_,
+    rs_,
+    rr_,
+):
+    n = seq_count
+    experts = seq_count * grp_count
+    tok = states_ref.shape[0]
+    width = states_ref.shape[1]
+    users, hist, hd = kbuf.shape[1:]
+    total = n * tok
+    me = lax.axis_index("seq")
+    mine = lax.axis_index("grp")
+    lin = me * grp_count + mine
+    loads = [
+        pltpu.make_async_copy(wo_ref, wo_v, wsem.at[0]),
+        pltpu.make_async_copy(up_ref.at[0], up_v, wsem.at[1]),
+        pltpu.make_async_copy(down_ref.at[0], down_v, wsem.at[2]),
+    ]
+
+    barrier = pltpu.get_barrier_semaphore()
+
+    def greet(d, carry):
+        peer = lax.rem(lin + d, experts)
+        pl.semaphore_signal(
+            barrier,
+            inc=1,
+            device_id={"seq": lax.div(peer, grp_count), "grp": lax.rem(peer, grp_count)},
+            device_id_type=MESH,
+        )
+        return carry
+
+    lax.fori_loop(1, experts, greet, 0)
+    pl.semaphore_wait(barrier, experts - 1)
+
+    def head_cols(index):
+        return pl.ds(pl.multiple_of(index * hd, hd), hd)
+
+    def tok_rows(index):
+        return pl.ds(pl.multiple_of(index * tok, tok), tok)
+
+    own = [
+        pltpu.make_async_copy(q_ref.at[:, head_cols(me)], qbuf.at[tok_rows(me)], lsem.at[0]),
+        pltpu.make_async_copy(k_ref.at[:, :, head_cols(me)], kbuf.at[0], lsem.at[1]),
+        pltpu.make_async_copy(v_ref.at[:, :, head_cols(me)], vbuf.at[0], lsem.at[2]),
+    ]
+    q_copies, k_copies, v_copies = [None], [None], [None]
+    for d in range(1, n):
+        peer = lax.rem(me + d, n)
+        to = dict(device_id={"seq": peer}, device_id_type=MESH)
+        q_copies.append(
+            pltpu.make_async_remote_copy(
+                q_ref.at[:, head_cols(peer)], qbuf.at[tok_rows(me)], qs.at[d], qr.at[d], **to
+            )
+        )
+        k_copies.append(
+            pltpu.make_async_remote_copy(
+                k_ref.at[:, :, head_cols(peer)], kbuf.at[d], ks.at[d], kr.at[d], **to
+            )
+        )
+        v_copies.append(
+            pltpu.make_async_remote_copy(
+                v_ref.at[:, :, head_cols(peer)], vbuf.at[d], vs.at[d], vr.at[d], **to
+            )
+        )
+    for copy in q_copies[1:] + k_copies[1:] + v_copies[1:]:
+        copy.start()
+    for copy in own:
+        copy.start()
+    for copy in loads:
+        copy.start()
+
+    pairs = rcol_ref.shape[0]
+    rcol, rrow = rcol_ref[...], rrow_ref[...]
+    same = rcol == rrow
+    up_i = lax.broadcasted_iota(jnp.int32, (pairs, pairs), 0)
+    low_i = lax.broadcasted_iota(jnp.int32, (pairs, pairs), 1)
+    slot_row = jnp.sum(jnp.where(same & (up_i < low_i), 1.0, 0.0), axis=0, keepdims=True)
+    slot_col = jnp.sum(jnp.where(same & (low_i < up_i), 1.0, 0.0), axis=1, keepdims=True)
+    rel_row = jnp.where(rrow >= lin, rrow - lin, rrow - lin + experts)
+    rel_col = jnp.where(rcol >= lin, rcol - lin, rcol - lin + experts)
+    target_row = rel_row * cap + slot_row.astype(jnp.int32)
+    target_col = rel_col * cap + slot_col.astype(jnp.int32)
+    top = pairs // tok
+
+    tile = 2 * tok
+    tiles = total // tile
+    factor = 1.0 / math.sqrt(hd)
+
+    def rows_of(t):
+        return pl.ds(pl.multiple_of(t * tile, tile), tile)
+
+    own[0].wait()
+    for copy in q_copies[1:]:
+        copy.wait_recv()
+    for d in range(n):
+        if d == 0:
+            own[1].wait()
+        else:
+            k_copies[d].wait_recv()
+        base = lax.rem(me - d + n, n) * hist
+
+        def score(t, carry, d=d, base=base):
+            rows = rows_of(t)
+            user = user_ref[rows, :]
+            keys = kbuf[d].reshape(users * hist, hd)
+            both = lax.dot_general(
+                qbuf[rows, :], keys, (((1,), (1,)), ((), ())), preferred_element_type=jnp.float32
+            )
+            picked = both[:, :hist]
+            limit = jnp.full(user.shape, lengths_ref[0], jnp.int32)
+            for member in range(1, users):
+                here = user == member
+                picked = jnp.where(here, both[:, member * hist : (member + 1) * hist], picked)
+                limit = jnp.where(here, lengths_ref[member], limit)
+            place = base + lax.broadcasted_iota(jnp.int32, (tile, hist), 1)
+            picked = jnp.where(place < limit, picked * factor, -1e30)
+            sbuf[d, rows, :] = picked
+            if d == 0:
+                mbuf[rows, :] = picked
+            else:
+                mbuf[rows, :] = jnp.maximum(mbuf[rows, :], picked)
+            return carry
+
+        lax.fori_loop(0, tiles, score, 0)
+
+    def soften(t, carry):
+        rows = rows_of(t)
+        user = user_ref[rows, :]
+        peak = jnp.max(mbuf[rows, :], axis=1, keepdims=True)
+        count = jnp.zeros((tile, hist), jnp.float32)
+        for d in range(n):
+            probs = jnp.exp(sbuf[d, rows, :] - peak)
+            count = count + probs
+            for member in range(users):
+                pbuf[d, rows, member * hist : (member + 1) * hist] = jnp.where(
+                    user == member, probs, 0.0
+                ).astype(jnp.bfloat16)
+        lbuf[rows, :] = jnp.broadcast_to(jnp.sum(count, axis=1, keepdims=True), (tile, hd))
+        return carry
+
+    lax.fori_loop(0, tiles, soften, 0)
+
+    for d in range(n):
+        if d == 0:
+            own[2].wait()
+        else:
+            v_copies[d].wait_recv()
+
+        def gather(t, carry, d=d):
+            rows = rows_of(t)
+            term = jnp.dot(
+                pbuf[d, rows, :],
+                vbuf[d].reshape(users * hist, hd),
+                preferred_element_type=jnp.float32,
+            )
+            if d > 0:
+                term = acc[rows, :] + term
+            if d < n - 1:
+                acc[rows, :] = term
+            else:
+                osend[rows, :] = (term / lbuf[rows, :]).astype(jnp.bfloat16)
+            return carry
+
+        lax.fori_loop(0, tiles, gather, 0)
+
+    o_copies = [None]
+    for d in range(1, n):
+        peer = lax.rem(me + d, n)
+        o_copies.append(
+            pltpu.make_async_remote_copy(
+                osend.at[tok_rows(peer)],
+                att.at[:, head_cols(me)],
+                os_.at[d],
+                or_.at[d],
+                device_id={"seq": peer},
+                device_id_type=MESH,
+            )
+        )
+        o_copies[d].start()
+    own_o = pltpu.make_async_copy(osend.at[tok_rows(me)], att.at[:, head_cols(me)], lsem.at[3])
+    own_o.start()
+    own_o.wait()
+    loads[0].wait()
+    for copy in o_copies[1:]:
+        copy.wait_recv()
+    residual = states_ref[...].astype(jnp.float32) + jnp.dot(
+        att[...], wo_v[...], preferred_element_type=jnp.float32
+    )
+    res[...] = residual
+    spread = jnp.mean(residual * residual, axis=-1, keepdims=True)
+    normed = (residual / jnp.sqrt(spread + 1e-06) * gain_ref[...]).astype(jnp.bfloat16)
+
+    per = min(experts, max(1, 128 // cap))
+    groups = experts // per
+    d_copies, r_copies = [None], [None]
+    for d in range(1, experts):
+        there = lax.rem(lin + d, experts)
+        back = lax.rem(lin - d + experts, experts)
+        d_copies.append(
+            pltpu.make_async_remote_copy(
+                dsend.at[d],
+                drecv.at[d],
+                ds_.at[d],
+                dr_.at[d],
+                device_id={"seq": lax.div(there, grp_count), "grp": lax.rem(there, grp_count)},
+                device_id_type=MESH,
+            )
+        )
+        r_copies.append(
+            pltpu.make_async_remote_copy(
+                rsend.at[d],
+                ans.at[d],
+                rs_.at[d],
+                rr_.at[d],
+                device_id={"seq": lax.div(back, grp_count), "grp": lax.rem(back, grp_count)},
+                device_id_type=MESH,
+            )
+        )
+    for group in range(groups):
+        place = lax.broadcasted_iota(jnp.int32, (per * cap, tok), 0) + group * per * cap
+        hit = place == target_row[:, :tok]
+        for k in range(1, top):
+            hit = hit | (place == target_row[:, k * tok : (k + 1) * tok])
+        rows = jnp.dot(
+            jnp.where(hit, 1.0, 0.0).astype(jnp.bfloat16), normed, preferred_element_type=jnp.float32
+        )
+        rows = rows.astype(jnp.bfloat16).reshape(per, cap, width)
+        dsend[group * per : (group + 1) * per] = rows
+        for d in range(group * per, (group + 1) * per):
+            if d > 0:
+                d_copies[d].start()
+    drecv[0] = dsend[0]
+
+    loads[1].wait()
+    loads[2].wait()
+    ff = up_v.shape[1]
+    step = min(ff, 512)
+    for group in range(groups):
+        for d in range(group * per, (group + 1) * per):
+            if d > 0:
+                d_copies[d].wait_recv()
+        facc[...] = jnp.zeros_like(facc)
+
+        def expert(j, carry, group=group):
+            cols = pl.ds(pl.multiple_of(j * step, step), step)
+            x = drecv[group * per : (group + 1) * per].reshape(per * cap, width)
+            hidden = jax.nn.gelu(
+                jnp.dot(x, up_v[:, cols], preferred_element_type=jnp.float32)
+            ).astype(jnp.bfloat16)
+            facc[...] += jnp.dot(hidden, down_v[cols, :], preferred_element_type=jnp.float32)
+            return carry
+
+        lax.fori_loop(0, ff // step, expert, 0)
+        rsend[group * per : (group + 1) * per] = (
+            facc[...].astype(jnp.bfloat16).reshape(per, cap, width)
+        )
+        for d in range(group * per, (group + 1) * per):
+            if d > 0:
+                r_copies[d].start()
+    ans[0] = rsend[0]
+
+    slots = experts * cap
+    lane = lax.broadcasted_iota(jnp.int32, (tok, slots), 1)
+    mix = jnp.zeros((tok, slots), jnp.float32)
+    for k in range(top):
+        span = slice(k * tok, (k + 1) * tok)
+        mix = mix + jnp.where(lane == target_col[span, :], rw_ref[span, :], 0.0)
+    high = mix.astype(jnp.bfloat16)
+    rest = (mix - high.astype(jnp.float32)).astype(jnp.bfloat16)
+    for copy in r_copies[1:]:
+        copy.wait_recv()
+    got = ans[...].reshape(slots, width)
+    mixed = jnp.dot(high, got, preferred_element_type=jnp.float32) + jnp.dot(
+        rest, got, preferred_element_type=jnp.float32
+    )
+    out_ref[...] = (res[...] + mixed).astype(jnp.bfloat16)
+    for copy in q_copies[1:] + k_copies[1:] + v_copies[1:] + o_copies[1:]:
+        copy.wait_send()
+    for copy in d_copies[1:] + r_copies[1:]:
+        copy.wait_send()
+
+
+def fused(
+    cap,
+    queries,
+    states,
+    behavior_keys,
+    behavior_values,
+    lengths,
+    user_of,
+    out_weight,
+    norm_gain,
+    routes,
+    route_weights,
+    expert_up,
+    expert_down,
+):
+    n = lax.axis_size("seq")
+    grp_count = lax.axis_size("grp")
+    experts = n * grp_count
+    tok, width = queries.shape
+    users, hist = behavior_keys.shape[:2]
+    ff = expert_up.shape[2]
+    hd = width // HEADS
+    total = n * tok
+    per = min(experts, max(1, 128 // cap))
+    bf, f32 = jnp.bfloat16, jnp.float32
+    vmem = pl.BlockSpec(memory_space=pltpu.VMEM)
+    hbm = pl.BlockSpec(memory_space=pl.ANY)
+    dma = pltpu.SemaphoreType.DMA
+    rflat = routes.T.reshape(-1)
+    return pl.pallas_call(
+        functools.partial(mega_kernel, n, grp_count, cap),
+        out_shape=jax.ShapeDtypeStruct((tok, width), bf),
+        in_specs=[pl.BlockSpec(memory_space=pltpu.SMEM)] + [hbm] * 6 + [vmem] * 6,
+        out_specs=vmem,
+        scratch_shapes=[
+            pltpu.VMEM((total, hd), bf),
+            pltpu.VMEM((n, users, hist, hd), bf),
+            pltpu.VMEM((n, users, hist, hd), bf),
+            pltpu.VMEM((n, total, hist), f32),
+            pltpu.VMEM((n, total, users * hist), bf),
+            pltpu.VMEM((total, hist), f32),
+            pltpu.VMEM((total, hd), f32),
+            pltpu.VMEM((total, hd), f32),
+            pltpu.VMEM((total, hd), bf),
+            pltpu.VMEM((tok, width), bf),
+            pltpu.VMEM((tok, width), f32),
+            pltpu.VMEM(out_weight.shape, bf),
+            pltpu.VMEM((width, ff), bf),
+            pltpu.VMEM((ff, width), bf),
+            pltpu.VMEM((experts, cap, width), bf),
+            pltpu.VMEM((experts, cap, width), bf),
+            pltpu.VMEM((experts, cap, width), bf),
+            pltpu.VMEM((experts, cap, width), bf),
+            pltpu.VMEM((per * cap, width), f32),
+            dma((3,)),
+            dma((4,)),
+        ]
+        + [dma((n,))] * 8
+        + [dma((experts,))] * 4,
+        compiler_params=pltpu.CompilerParams(
+            collective_id=0, has_side_effects=True, vmem_limit_bytes=58 * 2**20
+        ),
+    )(
+        lengths,
+        queries,
+        behavior_keys,
+        behavior_values,
+        expert_up,
+        expert_down,
+        out_weight,
+        user_of.reshape(total, 1),
+        states,
+        norm_gain.reshape(1, width),
+        rflat.reshape(-1, 1),
+        rflat.reshape(1, -1),
+        route_weights.T.reshape(-1, 1),
+    )
+
+
 def body(
     queries,
     states,
@@ -102,6 +515,24 @@
     expert_down,
 ):
     tok_count = queries.shape[0]
+    devices = lax.axis_size("seq") * lax.axis_size("grp")
+    room = max(2, 2 * tok_count * routes.shape[1] // devices)
+    if lax.axis_size("seq") == HEADS and room % 16 == 0:
+        return fused(
+            room,
+            queries,
+            states,
+            behavior_keys,
+            behavior_values,
+            lengths,
+            user_of,
+            out_weight,
+            norm_gain,
+            routes,
+            route_weights,
+            expert_up,
+            expert_down,
+        )
     attended = attend_heads(queries, behavior_keys, behavior_values, lengths, user_of)
     residual = states.astype(jnp.float32) + jnp.dot(
         attended, out_weight, preferred_element_type=jnp.float32

time: 196 us -> 142 us (0.72)
  Pallas kernels: 0 us -> 136 us
  waiting for transfers between devices: 79.4 us -> 0 us
  blocking collectives: 29.7 us -> 0 us
  matrix products: 26 us -> 0 us
  starting transfers between devices: 22.6 us -> 0 us
  local copies, waits for them, and re-layouts: 25.8 us -> 6.31 us
  other arithmetic: 11.3 us -> 0 us
    pallas_call x0 -> x1, Pallas kernels: none -> 136 us  [fused(): pl.pallas_call(functools.partial(mega_kernel, n, grp_count, cap), out_sha...]
    all_to_all x5 -> x0, waiting for transfers between devices: 79.4 us -> none  [the longest x1 25.9 us: body(): lax.all_to_all(received, ('seq', 'grp'), split_axis=0, concat_axis=0, til...]
    all_to_all x1 -> x0, blocking collectives: 29.7 us -> none  [body(): lax.all_to_all(buffer.reshape(experts_all, capacity, width), ('seq', 'grp...]
    dot_general x6 -> x0, matrix products: 26 us -> none  [the longest x1 16.1 us: body(): jnp.dot(hidden, expert_down[0], preferred_element_type=jnp.float32)]
    all_to_all x5 -> x0, starting transfers between devices: 22.6 us -> none  [the longest x1 7.32 us: attend_heads(): lax.all_to_all(query_send, 'seq', split_axis=0, concat_axis=0, tiled=True)]
    reduce_sum x3 -> x0, other arithmetic: 7.34 us -> none  [the longest x1 5.89 us: attend_heads(): total = probs.sum(-1, keepdims=True)]
    unnamed x27 -> x1, local copies, waits for them, and re-layouts: 6.74 us -> 1.67 us
    all_to_all x3 -> x0, local copies, waits for them, and re-layouts: 3.79 us -> none  [the longest x1 1.62 us: attend_heads(): lax.all_to_all(head_layout(behavior_keys, ratio), 'seq', split_axis=0, co...]
  transfers between devices with their start and end apart: 5 -> 0, of which waited for: 5 -> 0; matrix products, arithmetic and copies ran while one was open for 8% -> 0% of each run, Pallas kernels for 0% -> 0%
where the time goes in v2:
time: 142 us
  Pallas kernels  136 us (96%)
  local copies, waits for them, and re-layouts  6.31 us (4%)
    pallas_call x1, Pallas kernels, fused(): pl.pallas_call(functools.partial(mega_kernel, n, grp_count, cap), out_sha...  136 us

profile of v2, /device:TPU:0, one launch (start us, length us, event | category | flops | bytes accessed | tf_op | source)
XLA Modules:
  0.0 142.0 jit_solution(8133759670919040630)
XLA Ops:
  0.0 1.5 %copy.15.rw_ref = f32[256,1]{1,0:T(8,128)} copy(f32[256,1]{0,1:T(1,128)} %bitcast.14) | data formatting | bytes 2048 | tf_op jit(solution)/shard_map/reshape | solution.py:499
  1.5 1.5 %copy.14.rcol_ref = s32[256,1]{1,0:T(8,128)} copy(s32[256,1]{0,1:T(1,128)} %bitcast.11) | data formatting | bytes 2048 | tf_op jit(solution)/shard_map/reshape;reshape | solution.py:497
  2.9 1.7 %copy.13.user_ref = s32[1024,1]{1,0:T(8,128)} copy(s32[1024,1]{0,1:T(1,128)} %bitcast.10) | data formatting | bytes 8192 | tf_op jit(solution)/shard_map/reshape | solution.py:494
  4.6 135.7 %shard_map.118 = bf16[128,1024]{1,0:T(8,128)(2,1)} custom-call(s32[2]{0:T(128)} %lengths_ref.1, bf16[128,1024]{1,0:T(8,128)(2,1)} %q_ref.1, bf16[2,256,1024]{2,1,0:T(8,128)(2,1)} %k_ref.1, bf16[2,256,1024]{2,1,0:T(8,128)(2,1)} %v_ref.1, bf16[1,1024,4096]{2,1,0:T(8,128)(2,1)} %up_ref.1, bf16[1,4096,1024]{2,1,0:T(8,128)(2,1)} %down_ref.1, ...), custom_call_target="tpu_custom_call" | custom-call | tf_op jit(solution)/shard_map/pallas_call | solution.py:453
  140.3 1.7 %copy.17 = bf16[128,1024]{1,0:T(8,128)(2,1)} copy(bf16[128,1024]{1,0:T(8,128)(2,1)} %shard_map.118) | data formatting | bytes 524288
